TPU v7x, 32 devices: a whole 2x2x4 slice. The times are simulated.
32 devices in a mesh: seq: 4 (over z), uly: 4 (over y, x), rep: 2 (over core).
Axes of the slice: x: 2, y: 2, z: 4, core: 2. Of those that a mesh axis runs over, the one named last changes fastest.
Arguments:
- queries: bfloat16 [4096, 2048], P(('rep', 'seq', 'uly')), parts along dimension 0, may hold values from -6 to 6
- keys: bfloat16 [4096, 2048], P(('rep', 'seq', 'uly')), parts along dimension 0, may hold values from -6 to 6
- values: bfloat16 [4096, 2048], P(('rep', 'seq', 'uly')), parts along dimension 0, may hold values from -6 to 6
- past_outputs: bfloat16 [2, 4096, 2048], P(None, ('rep', 'seq', 'uly')), parts along dimension 1, may hold values from -6 to 6
- dwa_slot: int32 [2], replicated, may hold values from 0 to 63
- dwa_table: float32 [2, 64], replicated, may hold values from 0.1 to 0.6
Outputs:
- mixed: bfloat16 [4096, 2048], P(('rep', 'seq', 'uly')), parts along dimension 0
There are 2 independent parts, one for each index of `rep`. A program takes and returns all parts, laid end to end along the dimension named above; an argument that names none is the same for every part. Nothing has to cross between parts.
All inputs are finite; a program needn't handle non-finite values.
Results may differ from a plain program's by a relative error of at most 0.0034.
Values may be sent and summed in bfloat16 or wider, within the bound.
A program may use at most 64 MiB of HBM per device.

v0:
```python
import jax
import jax.numpy as jnp
from jax import lax
from jax.sharding import PartitionSpec as P

HEAD_DIM = 128


def from_behind(block, axis, distance):
    devices = range(lax.axis_size(axis))
    route = [(i - distance, i) for i in devices if i - distance in devices]
    return lax.ppermute(block, axis, route)


def block_update(state, query_heads, key_heads, value_heads, allowed):
    running, total, accumulated = state
    scores = jnp.einsum("qhd,khd->hqk", query_heads, key_heads, preferred_element_type=jnp.float32)
    scores = scores * (1.0 / HEAD_DIM**0.5)
    scores = jnp.where(allowed, scores, -jnp.inf)
    new_max = jnp.maximum(running, jnp.max(scores, axis=2))
    factor = jnp.exp(running - new_max)
    prob = jnp.exp(scores - new_max[:, :, None])
    total = total * factor + jnp.sum(prob, axis=2)
    weights = prob.astype(jnp.bfloat16)
    update = jnp.einsum("hqk,khd->qhd", weights, value_heads, preferred_element_type=jnp.float32)
    accumulated = accumulated * jnp.transpose(factor)[:, :, None] + update
    return (new_max, total, accumulated)


def shards(queries, keys, values, past_outputs, dwa_slot, dwa_table):
    n_uly = lax.axis_size("uly")
    n_seq = lax.axis_size("seq")
    span_size = min(4, n_seq)
    features = queries.shape[1]
    local_heads = features // n_uly // HEAD_DIM
    query_rows, key_rows, value_rows = (
        lax.all_to_all(queries, "uly", split_axis=1, concat_axis=0, tiled=True),
        lax.all_to_all(keys, "uly", split_axis=1, concat_axis=0, tiled=True),
        lax.all_to_all(values, "uly", split_axis=1, concat_axis=0, tiled=True),
    )
    row_count = query_rows.shape[0]
    split_shape = (row_count, local_heads, HEAD_DIM)
    query_heads = query_rows.reshape(split_shape)
    table_index = jnp.arange(dwa_table.shape[1])
    onehot = (dwa_slot[:, None] == table_index[None, :]).astype(jnp.float32)
    coefs = jnp.dot(onehot, jnp.transpose(dwa_table), precision=lax.Precision.HIGHEST)
    layer_in = jnp.zeros(queries.shape, jnp.float32)
    extra = jnp.zeros(queries.shape, jnp.float32)
    for index in range(past_outputs.shape[0]):
        stored = past_outputs[index].astype(jnp.float32)
        layer_in = layer_in + coefs[index, 0] * stored
        extra = extra + coefs[index, 1] * stored
    running = jnp.full((local_heads, row_count), -jnp.inf, jnp.float32)
    total = jnp.zeros((local_heads, row_count), jnp.float32)
    accumulated = jnp.zeros(split_shape, jnp.float32)
    state = (running, total, accumulated)
    causal = (jnp.arange(row_count)[:, None] >= jnp.arange(row_count)[None, :])[None, :, :]
    state = block_update(
        state, query_heads, key_rows.reshape(split_shape), value_rows.reshape(split_shape), causal
    )
    position = lax.axis_index("seq")
    current = (key_rows, value_rows)
    for offset in range(1, span_size):
        current = from_behind((current[0], current[1]), "seq", 1)
        far_keys = current[0].reshape(split_shape)
        far_values = current[1].reshape(split_shape)

        def take_block(carry, far_keys=far_keys, far_values=far_values):
            return block_update(carry, query_heads, far_keys, far_values, True)

        def keep_block(carry):
            return carry

        state = lax.cond(position >= offset, take_block, keep_block, state)
    running, total, accumulated = state
    attended = accumulated / jnp.transpose(total)[:, :, None]
    attended = attended.astype(jnp.bfloat16).reshape(row_count, local_heads * HEAD_DIM)
    returned = lax.all_to_all(attended, "uly", split_axis=0, concat_axis=1, tiled=True)
    hidden = layer_in + returned.astype(jnp.float32)
    return (hidden + extra).astype(jnp.bfloat16)


def solution(mesh):
    return jax.shard_map(
        shards,
        mesh=mesh,
        in_specs=(
            P(("rep", "seq", "uly"), None),
            P(("rep", "seq", "uly"), None),
            P(("rep", "seq", "uly"), None),
            P(None, ("rep", "seq", "uly"), None),
            P(),
            P(),
        ),
        out_specs=P(("rep", "seq", "uly"), None),
        check_vma=False,
    )
```

profile of v0, /device:TPU:24, one launch (start us, length us, event | category | flops | bytes accessed | tf_op | source)
XLA Modules:
  0.0 108.4 jit_solution(13092285454462107051)
XLA Ops:
  0.0 1.9 %copy.128 = bf16[16,4,8,512]{3,2,0,1:T(8,128)(2,1)} copy(bf16[16,4,8,512]{3,2,1,0:T(8,128)(2,1)} %bitcast.102) | data formatting | bytes 1048576 | tf_op jit(solution)/shard_map/all_to_all | solution.py:38
  1.9 3.7 %all-to-all-start.1 = ((bf16[128,4,512]{2,0,1:T(8,128)(2,1)}), bf16[128,4,512]{2,0,1:T(8,128)(2,1)S(1)}, u32[]{:S(2)}, u32[]{:S(2)}) async-start(bf16[128,4,512]{2,0,1:T(8,128)(2,1)} %bitcast.95), calls=%async_computation.1 | async-start | bytes 1048576 | tf_op jit(solution)/shard_map/all_to_all | solution.py:38
  5.7 1.9 %copy.127 = bf16[16,4,8,512]{3,2,0,1:T(8,128)(2,1)} copy(bf16[16,4,8,512]{3,2,1,0:T(8,128)(2,1)} %bitcast.103) | data formatting | bytes 1048576 | tf_op jit(solution)/shard_map/all_to_all | solution.py:39
  7.5 6.1 %all-to-all-done.1 = bf16[128,4,512]{2,0,1:T(8,128)(2,1)S(1)} async-done(((bf16[128,4,512]{2,0,1:T(8,128)(2,1)}), bf16[128,4,512]{2,0,1:T(8,128)(2,1)S(1)}, u32[]{:S(2)}, u32[]{:S(2)}) %all-to-all-start.1) | async-done | bytes 524320 | tf_op jit(solution)/shard_map/all_to_all | solution.py:38
  13.7 3.5 %all-to-all-start.2 = ((bf16[128,4,512]{2,0,1:T(8,128)(2,1)}), bf16[128,4,512]{2,0,1:T(8,128)(2,1)S(1)}, u32[]{:S(2)}, u32[]{:S(2)}) async-start(bf16[128,4,512]{2,0,1:T(8,128)(2,1)} %bitcast.94), calls=%async_computation.2 | async-start | bytes 1048576 | tf_op jit(solution)/shard_map/all_to_all | solution.py:39
  17.2 1.3 %collective-permute-start = (bf16[512,512]{1,0:T(8,128)(2,1)S(1)}, bf16[512,512]{1,0:T(8,128)(2,1)S(1)}, u32[]{:S(2)}, u32[]{:S(2)}) collective-permute-start(bf16[512,512]{1,0:T(8,128)(2,1)S(1)} %bitcast.99), channel_id=1, source_target_pairs={{0,8},{8,16},{16,24},{1,9},{9,17},{17,25},{2,10},{10,18},{18,26},{... | collective-permute-start | bytes 1572872 | tf_op jit(solution)/shard_map/ppermute | solution.py:12
  18.5 5.9 %all-to-all-done.2 = bf16[128,4,512]{2,0,1:T(8,128)(2,1)S(1)} async-done(((bf16[128,4,512]{2,0,1:T(8,128)(2,1)}), bf16[128,4,512]{2,0,1:T(8,128)(2,1)S(1)}, u32[]{:S(2)}, u32[]{:S(2)}) %all-to-all-start.2) | async-done | bytes 524320 | tf_op jit(solution)/shard_map/all_to_all | solution.py:39
  24.3 1.3 %collective-permute-start.1 = (bf16[512,512]{1,0:T(8,128)(2,1)S(1)}, bf16[512,512]{1,0:T(8,128)(2,1)}, u32[]{:S(2)}, u32[]{:S(2)}) collective-permute-start(bf16[512,512]{1,0:T(8,128)(2,1)S(1)} %bitcast.97), channel_id=1, source_target_pairs={{0,8},{8,16},{16,24},{1,9},{9,17},{17,25},{2,10},{10,18},{18,26},{... | collective-permute-start | bytes 1572872 | tf_op jit(solution)/shard_map/ppermute | solution.py:12
  25.6 0.8 copy.129
  26.5 3.5 %all-to-all-start = ((bf16[128,4,512]{2,0,1:T(8,128)(2,1)}), bf16[128,4,512]{2,0,1:T(8,128)(2,1)S(1)}, u32[]{:S(2)}, u32[]{:S(2)}) async-start(bf16[128,4,512]{2,0,1:T(8,128)(2,1)} %bitcast.96), calls=%async_computation | async-start | bytes 1048576 | tf_op jit(solution)/shard_map/all_to_all | solution.py:37
  30.1 6.4 %all-to-all-done = bf16[128,4,512]{2,0,1:T(8,128)(2,1)S(1)} async-done(((bf16[128,4,512]{2,0,1:T(8,128)(2,1)}), bf16[128,4,512]{2,0,1:T(8,128)(2,1)S(1)}, u32[]{:S(2)}, u32[]{:S(2)}) %all-to-all-start) | async-done | bytes 524320 | tf_op jit(solution)/shard_map/all_to_all | solution.py:37
  36.8 1.3 %collective-permute-start.2 = (bf16[512,512]{1,0:T(8,128)(2,1)S(1)}, bf16[512,512]{1,0:T(8,128)(2,1)}, u32[]{:S(2)}, u32[]{:S(2)}) collective-permute-start(bf16[512,512]{1,0:T(8,128)(2,1)S(1)} %collective-permute-done), channel_id=1, source_target_pairs={{0,8},{8,16},{16,24},{1,9},{9,17},{17,25},{2,10},{10,18},{18,26},{... | collective-permute-start | bytes 1572872 | tf_op jit(solution)/shard_map/ppermute | solution.py:12
  38.1 7.1 %collective-permute-done.1 = bf16[512,512]{1,0:T(8,128)(2,1)} collective-permute-done((bf16[512,512]{1,0:T(8,128)(2,1)S(1)}, bf16[512,512]{1,0:T(8,128)(2,1)}, u32[]{:S(2)}, u32[]{:S(2)}) %collective-permute-start.1) | collective-permute-done | bytes 524320 | tf_op jit(solution)/shard_map/ppermute | solution.py:12
  45.2 1.3 %collective-permute-start.3 = (bf16[512,512]{1,0:T(8,128)(2,1)}, bf16[512,512]{1,0:T(8,128)(2,1)}, u32[]{:S(2)}, u32[]{:S(2)}) collective-permute-start(bf16[512,512]{1,0:T(8,128)(2,1)} %collective-permute-done.1), channel_id=1, source_target_pairs={{0,8},{8,16},{16,24},{1,9},{9,17},{17,25},{2,10},{10,18},{18,26},{... | collective-permute-start | bytes 1572872 | tf_op jit(solution)/shard_map/ppermute | solution.py:12
  46.5 0.9 fusion.58
  47.4 1.9 %copy-done.1 = f32[4,512,512]{1,2,0:T(8,128)} copy-done((f32[4,512,512]{1,2,0:T(8,128)}, f32[4,512,512]{1,2,0:T(8,128)S(1)}, u32[]{:S(2)}) %copy-start.1) | copy-done | bytes 4194328
  49.4 0.9 fusion.60
  50.3 6.1 %collective-permute-done.2 = bf16[512,512]{1,0:T(8,128)(2,1)} collective-permute-done((bf16[512,512]{1,0:T(8,128)(2,1)S(1)}, bf16[512,512]{1,0:T(8,128)(2,1)}, u32[]{:S(2)}, u32[]{:S(2)}) %collective-permute-start.2) | collective-permute-done | bytes 524320 | tf_op jit(solution)/shard_map/ppermute | solution.py:12
  56.4 1.3 %collective-permute-start.4 = (bf16[512,512]{1,0:T(8,128)(2,1)}, bf16[512,512]{1,0:T(8,128)(2,1)S(1)}, u32[]{:S(2)}, u32[]{:S(2)}) collective-permute-start(bf16[512,512]{1,0:T(8,128)(2,1)} %collective-permute-done.2), channel_id=1, source_target_pairs={{0,8},{8,16},{16,24},{1,9},{9,17},{17,25},{2,10},{10,18},{18,26},{... | collective-permute-start | bytes 1572872 | tf_op jit(solution)/shard_map/ppermute | solution.py:12
  57.7 9.9 %collective-permute-done.3 = bf16[512,512]{1,0:T(8,128)(2,1)} collective-permute-done((bf16[512,512]{1,0:T(8,128)(2,1)}, bf16[512,512]{1,0:T(8,128)(2,1)}, u32[]{:S(2)}, u32[]{:S(2)}) %collective-permute-start.3) | collective-permute-done | bytes 524320 | tf_op jit(solution)/shard_map/ppermute | solution.py:12
  67.7 1.3 %collective-permute-start.5 = (bf16[512,512]{1,0:T(8,128)(2,1)}, bf16[512,512]{1,0:T(8,128)(2,1)}, u32[]{:S(2)}, u32[]{:S(2)}) collective-permute-start(bf16[512,512]{1,0:T(8,128)(2,1)} %collective-permute-done.3), channel_id=1, source_target_pairs={{0,8},{8,16},{16,24},{1,9},{9,17},{17,25},{2,10},{10,18},{18,26},{... | collective-permute-start | bytes 1572872 | tf_op jit(solution)/shard_map/ppermute | solution.py:12
  69.1 3.8 %fusion.70 = f32[512,4,128]{2,0,1:T(8,128)S(1)} fusion(f32[4,512,512]{1,2,0:T(8,128)} %copy-done.1, f32[4,512]{1,0:T(4,128)S(1)} %get-tuple-element.157, pred[512,512]{0,1:T(8,128)(4,1)S(1)} %iota_compare_fusion, bf16[512,4,128]{2,1,0:T(4,128)(2,1)S(1)} %reshape.86, f32[512,4]{0,1:T(4,128)S(1)} %get-tuple-element.151), kind=kOutput, calls=%fused_computation.66 | convolution fusion | flops 272891904 | bytes 6045696 | tf_op jit(solution)/shard_map/hqk,khd->qhd/dot_general | solution.py:25
  72.9 1.2 %reshape.87 = bf16[512,4,128]{2,1,0:T(4,128)(2,1)S(1)} reshape(bf16[512,512]{1,0:T(8,128)(2,1)} %copy-done.4) | data formatting | bytes 1048576 | tf_op jit(solution)/shard_map/reshape | solution.py:65
  74.0 1.2 %reshape.88 = bf16[512,4,128]{2,1,0:T(4,128)(2,1)S(1)} reshape(bf16[512,512]{1,0:T(8,128)(2,1)} %collective-permute-done.1) | data formatting | bytes 1048576 | tf_op jit(solution)/shard_map/reshape | solution.py:66
  75.2 2.9 %conditional.3 = ((f32[4,512]{1,0:T(4,128)S(1)}, f32[4,512]{1,0:T(4,128)S(1)}, f32[512,4,128]{2,0,1:T(8,128)S(1)})) conditional(s32[]{:T(128)} %convert_element_type.49, (f32[4,512]{1,0:T(4,128)S(1)}, f32[4,512]{1,0:T(4,128)S(1)}, f32[512,4,128]{2,0,1:T(8,128)S(1)}) %tuple.25, (bf16[512,4,128]{2,1,0:T(4,128)(2,1)S(1)}, ...), branch_computations={%region_2.3_spmd, %region_3.6_spmd} | conditional | flops 545789952 | bytes 16384032 | solution.py:74
  75.2 0.7 multiply_reduce_fusion
  76.0 0.7 fusion.1
  76.7 1.4 %fusion.9 = f32[512,4,128]{2,0,1:T(8,128)S(1)} fusion(f32[4,512,512]{1,2,0:T(8,128)S(1)} %get-tuple-element.144, f32[4,512]{1,0:T(4,128)S(1)} %get-tuple-element.162, f32[512,4,128]{2,0,1:T(8,128)S(1)} %get-tuple-element.65, bf16[512,4,128]{2,1,0:T(4,128)(2,1)S(1)} %get-tuple-element.124, f32[512,4]{0,1:T(4,128)S(1)} %get-tuple-element.137), kind=kOutput, calls=%fused_computation.8 | convolution fusion | flops 272105472 | bytes 6832128 | tf_op jit(solution)/shard_map/cond/branch_1_fun/hqk,khd->qhd/dot_general | solution.py:25
  78.2 5.0 %conditional.4 = ((f32[4,512]{1,0:T(4,128)S(1)}, f32[4,512]{1,0:T(4,128)S(1)}, f32[512,4,128]{2,0,1:T(8,128)S(1)})) conditional(s32[]{:T(128)} %convert_element_type.48, (f32[4,512]{1,0:T(4,128)S(1)}, f32[4,512]{1,0:T(4,128)S(1)}, f32[512,4,128]{2,0,1:T(8,128)S(1)}) %get-tuple-element.175, (bf16[512,512]{1,0:T(8,128)(2,1)}, ...), branch_computations={%region_6.7_spmd, %region_7.10_spmd} | conditional | flops 545789952 | bytes 16384032 | solution.py:74
  78.2 1.8 %multiply_reduce_fusion.1 = (f32[4,512]{1,0:T(4,128)S(1)}, f32[4,512,512]{1,2,0:T(8,128)S(1)}) fusion(bf16[512,4,128]{2,1,0:T(4,128)(2,1)S(1)} %get-tuple-element.126, bf16[512,512]{1,0:T(8,128)(2,1)} %get-tuple-element.69), kind=kOutput, calls=%fused_computation.18 | convolution fusion | flops 270530560 | bytes 5251072 | tf_op jit(solution)/shard_map/cond/branch_1_fun/qhd,khd->hqk/dot_general | solution.py:17
  80.0 0.7 fusion.19
  80.7 2.4 %fusion.27 = f32[512,4,128]{2,0,1:T(8,128)S(1)} fusion(f32[4,512,512]{1,2,0:T(8,128)S(1)} %get-tuple-element.146, f32[4,512]{1,0:T(4,128)S(1)} %get-tuple-element.168, f32[512,4,128]{2,0,1:T(8,128)S(1)} %get-tuple-element.71, f32[512,4]{0,1:T(4,128)S(1)} %get-tuple-element.139, bf16[512,512]{1,0:T(8,128)(2,1)} %get-tuple-element.72), kind=kOutput, calls=%fused_computation.25 | convolution fusion | flops 272105472 | bytes 6832128 | tf_op jit(solution)/shard_map/cond/branch_1_fun/hqk,khd->qhd/dot_general | solution.py:25
  83.1 4.8 %collective-permute-done.5 = bf16[512,512]{1,0:T(8,128)(2,1)} collective-permute-done((bf16[512,512]{1,0:T(8,128)(2,1)}, bf16[512,512]{1,0:T(8,128)(2,1)}, u32[]{:S(2)}, u32[]{:S(2)}) %collective-permute-start.5) | collective-permute-done | bytes 524320 | tf_op jit(solution)/shard_map/ppermute | solution.py:12
  87.9 3.9 %conditional.5 = ((f32[4,512]{1,0:T(4,128)S(1)}, f32[512,4,128]{2,0,1:T(8,128)S(1)})) conditional(s32[]{:T(128)} %convert_element_type.47, (f32[4,512]{1,0:T(4,128)S(1)}, f32[512,4,128]{2,0,1:T(8,128)S(1)}) %tuple.28, (bf16[512,512]{1,0:T(8,128)(2,1)S(1)}, bf16[512,4,128]{2,1,0:T(4,128)(2,1)S(1)}, f32[4,512]{1,0:T(4,128)S(1)}, ...), branch_computations={%region_10.11_spmd, %region_11.14_spmd} | conditional | flops 545789952 | bytes 16367640 | solution.py:74
  87.9 0.7 multiply_reduce_fusion.2
  88.7 0.7 fusion.39
  89.4 2.4 %fusion.47 = f32[512,4,128]{2,0,1:T(8,128)S(1)} fusion(f32[4,512,512]{1,2,0:T(8,128)S(1)} %get-tuple-element.148, f32[4,512]{1,0:T(4,128)S(1)} %get-tuple-element.142, f32[512,4,128]{2,0,1:T(8,128)S(1)} %get-tuple-element.77, f32[512,4]{0,1:T(4,128)S(1)} %get-tuple-element.141, bf16[512,512]{1,0:T(8,128)(2,1)} %get-tuple-element.78), kind=kOutput, calls=%fused_computation.44 | convolution fusion | flops 272105472 | bytes 6832128 | tf_op jit(solution)/shard_map/cond/branch_1_fun/hqk,khd->qhd/dot_general | solution.py:25
  91.9 0.3 divide_convert_fusion
  92.2 0.4 copy.60
  92.6 1.0 all_to_all.61
  93.6 3.9 %all-to-all-start.3 = ((bf16[4,128,512]{2,1,0:T(8,128)(2,1)}), bf16[4,128,512]{2,1,0:T(8,128)(2,1)S(1)}, u32[]{:S(2)}, u32[]{:S(2)}) async-start(bf16[4,128,512]{2,1,0:T(8,128)(2,1)} %all_to_all.61), calls=%async_computation.3 | async-start | bytes 1048576 | tf_op jit(solution)/shard_map/all_to_all | solution.py:78
  97.6 0.3 copy.67
  97.9 0.3 copy.68
  98.4 0.7 fusion.93
  99.0 5.0 %all-to-all-done.3 = bf16[4,128,512]{2,1,0:T(8,128)(2,1)S(1)} async-done(((bf16[4,128,512]{2,1,0:T(8,128)(2,1)}), bf16[4,128,512]{2,1,0:T(8,128)(2,1)S(1)}, u32[]{:S(2)}, u32[]{:S(2)}) %all-to-all-start.3) | async-done | bytes 524320 | tf_op jit(solution)/shard_map/all_to_all | solution.py:78
  104.2 0.3 copy.61
  104.5 2.8 %fusion.77 = bf16[128,2048]{0,1:T(8,128)(2,1)S(1)} fusion(bf16[1,128,2048]{1,2,0:T(8,128)(2,1)S(1)} %copy.67, bf16[1,128,2048]{1,2,0:T(8,128)(2,1)S(1)} %copy.68, f32[128,4,512]{0,2,1:T(8,128)S(1)} %copy.61, f32[]{:T(128)} %bitcast.20, f32[]{:T(128)} %bitcast.19, f32[]{:T(128)} %bitcast.7, f32[]{:T(128)} %bitcast.6), kind=kLoop, calls=%fused_computation.75 | loop fusion | flops 2883584 | bytes 2621456 | tf_op jit(solution)/shard_map/convert_element_type | solution.py:80
  107.4 1.0 copy.62
  (29 shorter events, 1.0 us)
Async XLA Ops:
  0.0 98.2 %copy-start = (f32[2,64]{1,0:T(2,128)S(1)}, f32[2,64]{1,0:T(2,128)}, u32[]{:S(2)}) copy-start(f32[2,64]{1,0:T(2,128)} %param.17) | copy-start | bytes 1540
  0.0 25.6 %copy-start.3 = (bf16[128,2048]{1,0:T(8,128)(2,1)S(1)}, bf16[128,2048]{1,0:T(8,128)(2,1)}, u32[]{:S(2)}) copy-start(bf16[128,2048]{1,0:T(8,128)(2,1)} %param.12) | copy-start | bytes 1572868
  1.9 11.7 %all-to-all-start.1 = ((bf16[128,4,512]{2,0,1:T(8,128)(2,1)}), bf16[128,4,512]{2,0,1:T(8,128)(2,1)S(1)}, u32[]{:S(2)}, u32[]{:S(2)}) async-start(bf16[128,4,512]{2,0,1:T(8,128)(2,1)} %bitcast.95), calls=%async_computation.1 | async-start | bytes 1048576 | tf_op jit(solution)/shard_map/all_to_all | solution.py:38
  13.7 10.7 %all-to-all-start.2 = ((bf16[128,4,512]{2,0,1:T(8,128)(2,1)}), bf16[128,4,512]{2,0,1:T(8,128)(2,1)S(1)}, u32[]{:S(2)}, u32[]{:S(2)}) async-start(bf16[128,4,512]{2,0,1:T(8,128)(2,1)} %bitcast.94), calls=%async_computation.2 | async-start | bytes 1048576 | tf_op jit(solution)/shard_map/all_to_all | solution.py:39
  17.2 19.6 %collective-permute-start = (bf16[512,512]{1,0:T(8,128)(2,1)S(1)}, bf16[512,512]{1,0:T(8,128)(2,1)S(1)}, u32[]{:S(2)}, u32[]{:S(2)}) collective-permute-start(bf16[512,512]{1,0:T(8,128)(2,1)S(1)} %bitcast.99), channel_id=1, source_target_pairs={{0,8},{8,16},{16,24},{1,9},{9,17},{17,25},{2,10},{10,18},{18,26},{... | collective-permute-start | bytes 1572872 | tf_op jit(solution)/shard_map/ppermute | solution.py:12
  24.3 20.9 %collective-permute-start.1 = (bf16[512,512]{1,0:T(8,128)(2,1)S(1)}, bf16[512,512]{1,0:T(8,128)(2,1)}, u32[]{:S(2)}, u32[]{:S(2)}) collective-permute-start(bf16[512,512]{1,0:T(8,128)(2,1)S(1)} %bitcast.97), channel_id=1, source_target_pairs={{0,8},{8,16},{16,24},{1,9},{9,17},{17,25},{2,10},{10,18},{18,26},{... | collective-permute-start | bytes 1572872 | tf_op jit(solution)/shard_map/ppermute | solution.py:12
  26.5 10.0 %all-to-all-start = ((bf16[128,4,512]{2,0,1:T(8,128)(2,1)}), bf16[128,4,512]{2,0,1:T(8,128)(2,1)S(1)}, u32[]{:S(2)}, u32[]{:S(2)}) async-start(bf16[128,4,512]{2,0,1:T(8,128)(2,1)} %bitcast.96), calls=%async_computation | async-start | bytes 1048576 | tf_op jit(solution)/shard_map/all_to_all | solution.py:37
  36.8 13.5 %copy-start.4 = (bf16[512,512]{1,0:T(8,128)(2,1)}, bf16[512,512]{1,0:T(8,128)(2,1)S(1)}, u32[]{:S(2)}) copy-start(bf16[512,512]{1,0:T(8,128)(2,1)S(1)} %collective-permute-done) | copy-start | bytes 1572868
  36.8 19.6 %collective-permute-start.2 = (bf16[512,512]{1,0:T(8,128)(2,1)S(1)}, bf16[512,512]{1,0:T(8,128)(2,1)}, u32[]{:S(2)}, u32[]{:S(2)}) collective-permute-start(bf16[512,512]{1,0:T(8,128)(2,1)S(1)} %collective-permute-done), channel_id=1, source_target_pairs={{0,8},{8,16},{16,24},{1,9},{9,17},{17,25},{2,10},{10,18},{18,26},{... | collective-permute-start | bytes 1572872 | tf_op jit(solution)/shard_map/ppermute | solution.py:12
  45.2 22.5 %collective-permute-start.3 = (bf16[512,512]{1,0:T(8,128)(2,1)}, bf16[512,512]{1,0:T(8,128)(2,1)}, u32[]{:S(2)}, u32[]{:S(2)}) collective-permute-start(bf16[512,512]{1,0:T(8,128)(2,1)} %collective-permute-done.1), channel_id=1, source_target_pairs={{0,8},{8,16},{16,24},{1,9},{9,17},{17,25},{2,10},{10,18},{18,26},{... | collective-permute-start | bytes 1572872 | tf_op jit(solution)/shard_map/ppermute | solution.py:12
  47.4 1.9 %copy-start.1 = (f32[4,512,512]{1,2,0:T(8,128)}, f32[4,512,512]{1,2,0:T(8,128)S(1)}, u32[]{:S(2)}) copy-start(f32[4,512,512]{1,2,0:T(8,128)S(1)} %get-tuple-element.158) | copy-start | bytes 12582916
  56.4 26.7 %collective-permute-start.4 = (bf16[512,512]{1,0:T(8,128)(2,1)}, bf16[512,512]{1,0:T(8,128)(2,1)S(1)}, u32[]{:S(2)}, u32[]{:S(2)}) collective-permute-start(bf16[512,512]{1,0:T(8,128)(2,1)} %collective-permute-done.2), channel_id=1, source_target_pairs={{0,8},{8,16},{16,24},{1,9},{9,17},{17,25},{2,10},{10,18},{18,26},{... | collective-permute-start | bytes 1572872 | tf_op jit(solution)/shard_map/ppermute | solution.py:12
  67.7 20.3 %collective-permute-start.5 = (bf16[512,512]{1,0:T(8,128)(2,1)}, bf16[512,512]{1,0:T(8,128)(2,1)}, u32[]{:S(2)}, u32[]{:S(2)}) collective-permute-start(bf16[512,512]{1,0:T(8,128)(2,1)} %collective-permute-done.3), channel_id=1, source_target_pairs={{0,8},{8,16},{16,24},{1,9},{9,17},{17,25},{2,10},{10,18},{18,26},{... | collective-permute-start | bytes 1572872 | tf_op jit(solution)/shard_map/ppermute | solution.py:12
  91.8 5.7 %copy-start.2 = (bf16[2,128,2048]{2,1,0:T(8,128)(2,1)S(1)}, bf16[2,128,2048]{2,1,0:T(8,128)(2,1)}, u32[]{:S(2)}) copy-start(bf16[2,128,2048]{2,1,0:T(8,128)(2,1)} %param.15) | copy-start | bytes 3145732
  91.9 6.3 %copy-start.5 = (s32[2]{0:T(128)S(1)}, s32[2]{0:T(128)}, u32[]{:S(2)}) copy-start(s32[2]{0:T(128)} %param.16) | copy-start | bytes 28
  93.6 10.4 %all-to-all-start.3 = ((bf16[4,128,512]{2,1,0:T(8,128)(2,1)}), bf16[4,128,512]{2,1,0:T(8,128)(2,1)S(1)}, u32[]{:S(2)}, u32[]{:S(2)}) async-start(bf16[4,128,512]{2,1,0:T(8,128)(2,1)} %all_to_all.61), calls=%async_computation.3 | async-start | bytes 1048576 | tf_op jit(solution)/shard_map/all_to_all | solution.py:78
where the time goes:
time: 109 us; the launch traced here: 108 us
  waiting for transfers between devices  51.5 us (47%)
  starting transfers between devices  22.2 us (20%)
  matrix products  14.4 us (13%)
  local copies, waits for them, and re-layouts  13.4 us (12%)
  other arithmetic  6.49 us (6%)
    ppermute x6, waiting for transfers between devices, from_behind(): return lax.ppermute(block, axis, route)  28 us
    dot_general x4, matrix products, block_update(): jnp.einsum('hqk,khd->qhd', weights, value_heads, preferred_element_type=j...  10.1 us
    ppermute x6, starting transfers between devices, from_behind(): return lax.ppermute(block, axis, route)  7.71 us
    all_to_all x1, waiting for transfers between devices, shards(): lax.all_to_all(queries, 'uly', split_axis=1, concat_axis=0, tiled=True)  6.45 us
    all_to_all x1, waiting for transfers between devices, shards(): lax.all_to_all(keys, 'uly', split_axis=1, concat_axis=0, tiled=True)  6.15 us
    all_to_all x1, waiting for transfers between devices, shards(): lax.all_to_all(values, 'uly', split_axis=1, concat_axis=0, tiled=True)  5.88 us
    all_to_all x1, waiting for transfers between devices, shards(): lax.all_to_all(attended, 'uly', split_axis=0, concat_axis=1, tiled=True)  5.04 us
    dot_general x4, matrix products, block_update(): jnp.einsum('qhd,khd->hqk', query_heads, key_heads, preferred_element_type...  4.16 us
  transfers between devices with their start and end apart: 10, of which 8 were waited for; matrix products, arithmetic and copies ran while one was open for 19% of the time, Pallas kernels for 0%

commit v1 on v0

--- a/solution.py
+++ b/solution.py
@@ -1,9 +1,18 @@
+import functools
+import math
+
 import jax
 import jax.numpy as jnp
 from jax import lax
+from jax.experimental import pallas as pl
+from jax.experimental.pallas import tpu as pltpu
 from jax.sharding import PartitionSpec as P
 
 HEAD_DIM = 128
+SPAN = 4
+STAT = 16
+MESH = pl.DeviceIdType.MESH
+Q, K, V = 0, 1, 2
 
 
 def from_behind(block, axis, distance):
@@ -80,9 +89,396 @@
     return (hidden + extra).astype(jnp.bfloat16)
 
 
+def fused_kernel(
+    shape,
+    slot_ref, table_ref, q_hbm, k_hbm, v_hbm, past_hbm, out_ref,
+    given, past, heads, own, own_stat, part_out, part_in, att, back,
+    load_sem, past_sem, plane_sem, line_sem, heads_sem, part_send, part_recv, att_sem, back_sem,
+):
+    n_seq, n_uly, group = shape
+    tokens = given.shape[1]
+    rows = n_uly * tokens
+    half = rows // 2
+    scale = math.log2(math.e) / HEAD_DIM**0.5
+    s, t = lax.axis_index("seq"), lax.axis_index("uly")
+    alone = group - 1
+    shared = group - 1
+
+    loads = [
+        pltpu.make_async_copy(src, given.at[i], load_sem.at[i]) for i, src in enumerate((q_hbm, k_hbm, v_hbm))
+    ]
+    for load in loads:
+        load.start()
+    past_load = pltpu.make_async_copy(past_hbm, past, past_sem)
+    past_load.start()
+
+    barrier = pltpu.get_barrier_semaphore()
+    for d in range(1, n_uly):
+        pl.semaphore_signal(barrier, inc=1, device_id={"uly": lax.rem(t + d, n_uly)}, device_id_type=MESH)
+    for d in range(1, n_seq):
+        pl.semaphore_signal(barrier, inc=1, device_id={"seq": lax.rem(s + d, n_seq)}, device_id_type=MESH)
+
+    @pl.when(s == 3)
+    def _():
+        for d in range(1, n_uly):
+            pl.semaphore_signal(
+                barrier, inc=1, device_id={"seq": 2, "uly": lax.rem(t + d, n_uly)}, device_id_type=MESH
+            )
+
+    pl.semaphore_wait(barrier, n_uly + n_seq - 2 + jnp.where(s == 2, n_uly - 1, 0))
+    for load in loads:
+        load.wait()
+
+    def columns(uly, g):
+        return pl.ds(pl.multiple_of((uly * group + g) * HEAD_DIM, HEAD_DIM), HEAD_DIM)
+
+    my_rows = pl.ds(pl.multiple_of(t * tokens, tokens), tokens)
+
+    def plane(kind, g, d):
+        peer = lax.rem(t + d, n_uly)
+        src = given.at[kind, :, columns(peer, g)]
+        dst = heads.at[kind, g, s, my_rows, :]
+        if d == 0:
+            return pltpu.make_async_copy(src, dst, heads_sem.at[kind, g, s])
+        return pltpu.make_async_remote_copy(
+            src, dst, plane_sem.at[kind, g, d], heads_sem.at[kind, g, s],
+            device_id={"uly": peer}, device_id_type=MESH,
+        )
+
+    def scatter(kind, g):
+        for d in (*range(1, n_uly), 0):
+            plane(kind, g, d).start()
+
+    def arrived(kind, g, block):
+        ref = heads.at[kind, g, block]
+        pltpu.make_async_copy(ref, ref, heads_sem.at[kind, g, block]).wait()
+
+    def line(kind, g, to, lane=0):
+        ref = heads.at[kind, g, s]
+        return pltpu.make_async_remote_copy(
+            ref, ref, line_sem.at[kind, g, lane], heads_sem.at[kind, g, s],
+            device_id={"seq": to}, device_id_type=MESH,
+        )
+
+    def partial(g, block):
+        return pltpu.make_async_remote_copy(
+            part_out.at[g, block - n_seq // 2], part_in.at[g],
+            part_send.at[g, block - n_seq // 2], part_recv.at[g],
+            device_id={"seq": block}, device_id_type=MESH,
+        )
+
+    def returning(g, lane, block, d):
+        peer = lax.rem(t + d, n_uly)
+        src = att.at[lane, g, pl.ds(pl.multiple_of(peer * tokens, tokens), tokens), :]
+        dst = back.at[:, columns(t, g)]
+        if block is None and d == 0:
+            return pltpu.make_async_copy(src, dst, back_sem.at[g, t])
+        where = {"uly": peer} if block is None else {"seq": block, "uly": peer}
+        return pltpu.make_async_remote_copy(
+            src, dst, att_sem.at[lane, g, d], back_sem.at[g, t], device_id=where, device_id_type=MESH,
+        )
+
+    def give_back(g, lane=0, block=None):
+        for d in (*range(1, n_uly), 0):
+            returning(g, lane, block, d).start()
+
+    def attend(g, block, full, diagonal, finish):
+        for a in range(2):
+            query = heads[Q, g, block, a * half:(a + 1) * half, :]
+            top = total = acc = None
+            spans = [(j, rows, False) for j in full] + ([(block, (a + 1) * half, True)] if diagonal else [])
+            for j, count, masked in spans:
+                key = heads[K, g, j, 0:count, :]
+                value = heads[V, g, j, 0:count, :]
+                scores = lax.dot_general(key, query, (((1,), (1,)), ((), ())), preferred_element_type=jnp.float32)
+                scores = scores * scale
+                if masked:
+                    key_at = lax.broadcasted_iota(jnp.int32, scores.shape, 0)
+                    query_at = lax.broadcasted_iota(jnp.int32, scores.shape, 1) + a * half
+                    scores = jnp.where(key_at <= query_at, scores, -jnp.inf)
+                peak = jnp.max(scores, axis=0, keepdims=True)
+                new_top = peak if top is None else jnp.maximum(top, peak)
+                prob = jnp.exp2(scores - new_top)
+                sums = jnp.sum(prob, axis=0, keepdims=True)
+                update = lax.dot_general(
+                    value, prob.astype(jnp.bfloat16), (((0,), (0,)), ((), ())), preferred_element_type=jnp.float32
+                )
+                if top is None:
+                    total, acc = sums, update
+                else:
+                    factor = jnp.exp2(top - new_top)
+                    total = total * factor + sums
+                    acc = acc * factor + update
+                top = new_top
+            finish(slice(a * half, (a + 1) * half), top, total, acc)
+
+    def settle(g, lane=0):
+        def finish(cut, top, total, acc):
+            att[lane, g, cut, :] = jnp.transpose(acc / total).astype(jnp.bfloat16)
+        return finish
+
+    def keep(g):
+        def finish(cut, top, total, acc):
+            own[g, :, cut] = acc
+            own_stat[g, 0:1, cut] = top
+            own_stat[g, 1:2, cut] = total
+        return finish
+
+    def hand_over(g, where):
+        def finish(cut, top, total, acc):
+            part_out[g, where, 0:HEAD_DIM, cut] = (acc / total).astype(jnp.bfloat16)
+            level = top + jnp.log2(total)
+            high = level.astype(jnp.bfloat16).astype(jnp.float32)
+            middle = (level - high).astype(jnp.bfloat16).astype(jnp.float32)
+            low = level - high - middle
+            row = lax.broadcasted_iota(jnp.int32, (STAT, half), 0)
+            stats = jnp.where(row == 0, high, jnp.where(row == 1, middle, jnp.where(row == 2, low, 0.0)))
+            part_out[g, where, HEAD_DIM:HEAD_DIM + STAT, cut] = stats.astype(jnp.bfloat16)
+        return finish
+
+    def merge(g):
+        pltpu.make_async_copy(part_in.at[g], part_in.at[g], part_recv.at[g]).wait()
+        for a in range(2):
+            cut = slice(a * half, (a + 1) * half)
+            stats = part_in[g, HEAD_DIM:HEAD_DIM + STAT, cut].astype(jnp.float32)
+            level = stats[0:1] + stats[1:2] + stats[2:3]
+            top, total = own_stat[g, 0:1, cut], own_stat[g, 1:2, cut]
+            new_top = jnp.maximum(top, level)
+            mine, theirs = jnp.exp2(top - new_top), jnp.exp2(level - new_top)
+            inverse = 1.0 / (total * mine + theirs)
+            other = part_in[g, 0:HEAD_DIM, cut].astype(jnp.float32)
+            both = own[g, :, cut] * (mine * inverse) + other * (theirs * inverse)
+            att[0, g, cut, :] = jnp.transpose(both).astype(jnp.bfloat16)
+
+    def each(count, body):
+        def step(g, carry):
+            body(g)
+            return carry
+        lax.fori_loop(0, count, step, 0)
+
+    every = (alone, *range(shared))
+
+    @pl.when(s == 0)
+    def _():
+        for g in every:
+            scatter(K, g)
+            scatter(V, g)
+        for g in every:
+            scatter(Q, g)
+        for g in every:
+            for kind in (K, V):
+                arrived(kind, g, 0)
+                if g == alone:
+                    line(kind, g, 2, 1).start()
+                else:
+                    line(kind, g, 1).start()
+        for kind in (K, V):
+            line(kind, alone, 1).start()
+
+        def work(g):
+            arrived(Q, g, 0)
+            attend(g, 0, (), True, settle(g))
+            give_back(g)
+        each(group, work)
+
+    @pl.when(s == 1)
+    def _():
+        for g in every:
+            scatter(K, g)
+            scatter(V, g)
+        for g in every:
+            scatter(Q, g)
+        for kind in (K, V):
+            arrived(kind, alone, 1)
+            line(kind, alone, 2).start()
+
+        def far(g):
+            for kind in (K, V):
+                arrived(kind, g, 1)
+                arrived(kind, g, 0)
+            for block in (2, 3):
+                arrived(Q, g, block)
+                attend(g, block, (0, 1), False, hand_over(g, block - n_seq // 2))
+                partial(g, block).start()
+        each(shared, far)
+        for kind in (K, V):
+            arrived(kind, alone, 0)
+
+        def near(g):
+            arrived(Q, g, 1)
+            attend(g, 1, (0,), True, settle(g))
+            give_back(g)
+        each(group, near)
+
+    @pl.when(s == 2)
+    def _():
+        for g in range(shared):
+            scatter(Q, g)
+        for g in range(shared):
+            scatter(K, g)
+            scatter(V, g)
+        for kind in (Q, K, V):
+            scatter(kind, alone)
+        for g in range(shared):
+            arrived(Q, g, 2)
+            line(Q, g, 1).start()
+        for g in range(shared):
+            for kind in (K, V):
+                arrived(kind, g, 2)
+                line(kind, g, 3).start()
+
+        def near(g):
+            attend(g, 2, (), True, keep(g))
+        each(shared, near)
+        for kind in (Q, K, V):
+            arrived(kind, alone, 2)
+        for kind in (K, V):
+            arrived(kind, alone, 0)
+            arrived(kind, alone, 1)
+        attend(alone, 2, (0, 1), True, settle(alone))
+        give_back(alone)
+        for kind in (Q, K, V):
+            arrived(kind, alone, 3)
+        attend(alone, 3, (0, 1, 2), True, settle(alone, 1))
+        give_back(alone, 1, 3)
+
+        def join(g):
+            merge(g)
+            give_back(g)
+        each(shared, join)
+
+    @pl.when(s == 3)
+    def _():
+        for g in range(shared):
+            scatter(Q, g)
+        for kind in (Q, K, V):
+            scatter(kind, alone)
+        for g in range(shared):
+            scatter(K, g)
+            scatter(V, g)
+        for g in range(shared):
+            arrived(Q, g, 3)
+            line(Q, g, 1).start()
+        for kind in (Q, K, V):
+            arrived(kind, alone, 3)
+            line(kind, alone, 2).start()
+
+        def near(g):
+            for kind in (K, V):
+                arrived(kind, g, 3)
+                arrived(kind, g, 2)
+            attend(g, 3, (2,), True, keep(g))
+        each(shared, near)
+
+        def join(g):
+            merge(g)
+            give_back(g)
+        each(shared, join)
+
+    past_load.wait()
+    weights = [table_ref[0, slot_ref[p]] + table_ref[1, slot_ref[p]] for p in range(past.shape[0])]
+
+    def combine(g):
+        for uly in range(n_uly):
+            cols = columns(uly, g)
+            pltpu.make_async_copy(back.at[:, cols], back.at[:, cols], back_sem.at[g, uly]).wait()
+            mixed = back[:, cols].astype(jnp.float32)
+            for p, weight in enumerate(weights):
+                mixed = mixed + weight * past[p, :, cols].astype(jnp.float32)
+            out_ref[:, cols] = mixed.astype(out_ref.dtype)
+    each(group, combine)
+
+    for g in range(group):
+        for d in range(1, n_uly):
+            for kind in (Q, K, V):
+                plane(kind, g, d).wait_send()
+
+    def returned(g, lane=0, block=None):
+        for d in range(0 if block is not None else 1, n_uly):
+            returning(g, lane, block, d).wait_send()
+
+    @pl.when(s == 0)
+    def _():
+        for g in range(group):
+            for kind in (K, V):
+                line(kind, g, 1).wait_send()
+            returned(g)
+        for kind in (K, V):
+            line(kind, alone, 2, 1).wait_send()
+
+    @pl.when(s == 1)
+    def _():
+        for kind in (K, V):
+            line(kind, alone, 2).wait_send()
+        for g in range(shared):
+            for block in (2, 3):
+                partial(g, block).wait_send()
+        for g in range(group):
+            returned(g)
+
+    @pl.when(s == 2)
+    def _():
+        for g in range(shared):
+            line(Q, g, 1).wait_send()
+            for kind in (K, V):
+                line(kind, g, 3).wait_send()
+        for g in range(group):
+            returned(g)
+        returned(alone, 1, 3)
+
+    @pl.when(s == 3)
+    def _():
+        for g in range(shared):
+            line(Q, g, 1).wait_send()
+            returned(g)
+        for kind in (Q, K, V):
+            line(kind, alone, 2).wait_send()
+
+
+def fused(queries, keys, values, past_outputs, dwa_slot, dwa_table):
+    n_seq, n_uly = lax.axis_size("seq"), lax.axis_size("uly")
+    tokens, features = queries.shape
+    group = features // n_uly // HEAD_DIM
+    rows = tokens * n_uly
+    stored = past_outputs.shape[0]
+    bf16, f32 = jnp.bfloat16, jnp.float32
+    anywhere = pl.BlockSpec(memory_space=pl.ANY)
+    scalars = pl.BlockSpec(memory_space=pltpu.SMEM)
+    return pl.pallas_call(
+        functools.partial(fused_kernel, (n_seq, n_uly, group)),
+        out_shape=jax.ShapeDtypeStruct((tokens, features), bf16),
+        in_specs=[scalars, scalars, anywhere, anywhere, anywhere, anywhere],
+        out_specs=pl.BlockSpec(memory_space=pltpu.VMEM),
+        scratch_shapes=[
+            pltpu.VMEM((3, tokens, features), bf16),
+            pltpu.VMEM((stored, tokens, features), bf16),
+            pltpu.VMEM((3, group, n_seq, rows, HEAD_DIM), bf16),
+            pltpu.VMEM((group, HEAD_DIM, rows), f32),
+            pltpu.VMEM((group, 8, rows), f32),
+            pltpu.VMEM((group, 2, HEAD_DIM + STAT, rows), bf16),
+            pltpu.VMEM((group, HEAD_DIM + STAT, rows), bf16),
+            pltpu.VMEM((2, group, rows, HEAD_DIM), bf16),
+            pltpu.VMEM((tokens, features), bf16),
+            pltpu.SemaphoreType.DMA((3,)),
+            pltpu.SemaphoreType.DMA,
+            pltpu.SemaphoreType.DMA((3, group, n_uly)),
+            pltpu.SemaphoreType.DMA((3, group, 2)),
+            pltpu.SemaphoreType.DMA((3, group, n_seq)),
+            pltpu.SemaphoreType.DMA((group, 2)),
+            pltpu.SemaphoreType.DMA((group,)),
+            pltpu.SemaphoreType.DMA((2, group, n_uly)),
+            pltpu.SemaphoreType.DMA((group, n_uly)),
+        ],
+        compiler_params=pltpu.CompilerParams(
+            collective_id=0, has_side_effects=True, vmem_limit_bytes=48 * 1024 * 1024
+        ),
+    )(dwa_slot, dwa_table, queries, keys, values, past_outputs)
+
+
 def solution(mesh):
+    body = fused if mesh.shape["seq"] == SPAN else shards
     return jax.shard_map(
-        shards,
+        body,
         mesh=mesh,
         in_specs=(
             P(("rep", "seq", "uly"), None),

time: 109 us -> 55.3 us (0.51)
  waiting for transfers between devices: 51.5 us -> 0 us
  Pallas kernels: 0 us -> 48 us
  starting transfers between devices: 22.2 us -> 0 us
  matrix products: 14.4 us -> 0 us
  local copies, waits for them, and re-layouts: 13.4 us -> 6.48 us
  other arithmetic: 6.49 us -> 0 us
    pallas_call x0 -> x1, Pallas kernels: none -> 48 us  [fused(): pl.pallas_call(functools.partial(fused_kernel, (n_seq, n_uly, group)), ou...]
    ppermute x6 -> x0, waiting for transfers between devices: 28 us -> none  [from_behind(): return lax.ppermute(block, axis, route)]
    all_to_all x4 -> x0, waiting for transfers between devices: 23.5 us -> none  [the longest x1 6.45 us: shards(): lax.all_to_all(queries, 'uly', split_axis=1, concat_axis=0, tiled=True)]
    all_to_all x4 -> x0, starting transfers between devices: 14.5 us -> none  [the longest x1 3.87 us: shards(): lax.all_to_all(attended, 'uly', split_axis=0, concat_axis=1, tiled=True)]
    dot_general x9 -> x0, matrix products: 14.4 us -> none  [the longest x4 10.1 us: block_update(): jnp.einsum('hqk,khd->qhd', weights, value_heads, preferred_element_type=j...]
    ppermute x6 -> x0, starting transfers between devices: 7.71 us -> none  [from_behind(): return lax.ppermute(block, axis, route)]
    all_to_all x4 -> x0, local copies, waits for them, and re-layouts: 5.65 us -> none  [the longest x1 1.94 us: shards(): lax.all_to_all(keys, 'uly', split_axis=1, concat_axis=0, tiled=True)]
    unnamed x14 -> x13, local copies, waits for them, and re-layouts: 2.52 us -> 6.48 us
  transfers between devices with their start and end apart: 10 -> 0, of which waited for: 8 -> 0; matrix products, arithmetic and copies ran while one was open for 19% -> 0% of each run, Pallas kernels for 0% -> 0%
where the time goes in v1:
time: 55.3 us; the launch traced here: 54.5 us
  Pallas kernels  48 us (87%)
  local copies, waits for them, and re-layouts  6.48 us (12%)
    pallas_call x1, Pallas kernels, fused(): pl.pallas_call(functools.partial(fused_kernel, (n_seq, n_uly, group)), ou...  48 us
    unnamed x13, local copies, waits for them, and re-layouts  6.48 us

profile of v1, /device:TPU:24, one launch (start us, length us, event | category | flops | bytes accessed | tf_op | source)
XLA Modules:
  0.0 54.5 jit_solution(15753062489608658476)
XLA Ops:
  0.0 0.0 copy-start
  0.0 1.2 %copy-done = bf16[2,128,2048]{2,1,0:T(8,128)(2,1)S(1)} copy-done((bf16[2,128,2048]{2,1,0:T(8,128)(2,1)S(1)}, bf16[2,128,2048]{2,1,0:T(8,128)(2,1)}, u32[]{:S(2)}) %copy-start) | copy-done | bytes 1048600
  1.2 0.0 copy-start.1
  1.2 1.0 %copy-done.1 = bf16[128,2048]{1,0:T(8,128)(2,1)S(1)} copy-done((bf16[128,2048]{1,0:T(8,128)(2,1)S(1)}, bf16[128,2048]{1,0:T(8,128)(2,1)}, u32[]{:S(2)}) %copy-start.1) | copy-done | bytes 524312
  2.3 0.0 copy-start.2
  2.3 1.0 %copy-done.2 = bf16[128,2048]{1,0:T(8,128)(2,1)S(1)} copy-done((bf16[128,2048]{1,0:T(8,128)(2,1)S(1)}, bf16[128,2048]{1,0:T(8,128)(2,1)}, u32[]{:S(2)}) %copy-start.2) | copy-done | bytes 524312
  3.3 0.0 copy-start.3
  3.3 1.0 %copy-done.3 = bf16[128,2048]{1,0:T(8,128)(2,1)S(1)} copy-done((bf16[128,2048]{1,0:T(8,128)(2,1)S(1)}, bf16[128,2048]{1,0:T(8,128)(2,1)}, u32[]{:S(2)}) %copy-start.3) | copy-done | bytes 524312
  4.4 0.0 copy-start.4
  4.4 0.7 %copy-done.4 = f32[2,64]{1,0:T(2,128)S(1)} copy-done((f32[2,64]{1,0:T(2,128)S(1)}, f32[2,64]{1,0:T(2,128)}, u32[]{:S(2)}) %copy-start.4) | copy-done | bytes 536
  5.0 0.0 copy-start.5
  5.0 0.7 %copy-done.5 = s32[2]{0:T(128)S(1)} copy-done((s32[2]{0:T(128)S(1)}, s32[2]{0:T(128)}, u32[]{:S(2)}) %copy-start.5) | copy-done | bytes 32
  5.7 48.0 %shard_map.64 = bf16[128,2048]{1,0:T(8,128)(2,1)S(1)} custom-call(s32[2]{0:T(128)S(1)} %copy-done.5, f32[2,64]{1,0:T(2,128)S(1)} %copy-done.4, bf16[128,2048]{1,0:T(8,128)(2,1)S(1)} %copy-done.1, bf16[128,2048]{1,0:T(8,128)(2,1)S(1)} %copy-done.2, bf16[128,2048]{1,0:T(8,128)(2,1)S(1)} %copy-done.3, bf16[2,128,2048]{2,1,0:T(8,128)(2,1)S(1)} %copy-done), custom_call_target="tpu_custom_call" | custom-call | tf_op jit(solution)/shard_map/pallas_call | solution.py:447
  53.7 0.8 %copy.8 = bf16[128,2048]{1,0:T(8,128)(2,1)} copy(bf16[128,2048]{1,0:T(8,128)(2,1)S(1)} %shard_map.64) | data formatting | bytes 1048576
Async XLA Ops:
  0.0 1.2 %copy-start = (bf16[2,128,2048]{2,1,0:T(8,128)(2,1)S(1)}, bf16[2,128,2048]{2,1,0:T(8,128)(2,1)}, u32[]{:S(2)}) copy-start(bf16[2,128,2048]{2,1,0:T(8,128)(2,1)} %past_hbm.1) | copy-start | bytes 3145732
  1.2 1.0 %copy-start.1 = (bf16[128,2048]{1,0:T(8,128)(2,1)S(1)}, bf16[128,2048]{1,0:T(8,128)(2,1)}, u32[]{:S(2)}) copy-start(bf16[128,2048]{1,0:T(8,128)(2,1)} %q_hbm.1) | copy-start | bytes 1572868
  2.3 1.0 %copy-start.2 = (bf16[128,2048]{1,0:T(8,128)(2,1)S(1)}, bf16[128,2048]{1,0:T(8,128)(2,1)}, u32[]{:S(2)}) copy-start(bf16[128,2048]{1,0:T(8,128)(2,1)} %k_hbm.1) | copy-start | bytes 1572868
  3.3 1.0 %copy-start.3 = (bf16[128,2048]{1,0:T(8,128)(2,1)S(1)}, bf16[128,2048]{1,0:T(8,128)(2,1)}, u32[]{:S(2)}) copy-start(bf16[128,2048]{1,0:T(8,128)(2,1)} %v_hbm.1) | copy-start | bytes 1572868
  4.4 0.7 %copy-start.4 = (f32[2,64]{1,0:T(2,128)S(1)}, f32[2,64]{1,0:T(2,128)}, u32[]{:S(2)}) copy-start(f32[2,64]{1,0:T(2,128)} %table_ref.1) | copy-start | bytes 1540
  5.0 0.7 %copy-start.5 = (s32[2]{0:T(128)S(1)}, s32[2]{0:T(128)}, u32[]{:S(2)}) copy-start(s32[2]{0:T(128)} %slot_ref.1) | copy-start | bytes 28

commit v2 on v1

--- a/solution.py
+++ b/solution.py
@@ -103,6 +103,8 @@
     s, t = lax.axis_index("seq"), lax.axis_index("uly")
     alone = group - 1
     shared = group - 1
+    guest = 0
+    late, visit = group, group + 1
 
     loads = [
         pltpu.make_async_copy(src, given.at[i], load_sem.at[i]) for i, src in enumerate((q_hbm, k_hbm, v_hbm))
@@ -153,18 +155,20 @@
         ref = heads.at[kind, g, block]
         pltpu.make_async_copy(ref, ref, heads_sem.at[kind, g, block]).wait()
 
-    def line(kind, g, to, lane=0):
-        ref = heads.at[kind, g, s]
+    def line(kind, g, to, lane=0, block=None):
+        block = s if block is None else block
+        ref = heads.at[kind, g, block]
         return pltpu.make_async_remote_copy(
-            ref, ref, line_sem.at[kind, g, lane], heads_sem.at[kind, g, s],
+            ref, ref, line_sem.at[kind, g, lane], heads_sem.at[kind, g, block],
             device_id={"seq": to}, device_id_type=MESH,
         )
 
-    def partial(g, block):
+    def partial(g, block, to=None, slot=None):
+        slot = g if slot is None else slot
         return pltpu.make_async_remote_copy(
-            part_out.at[g, block - n_seq // 2], part_in.at[g],
-            part_send.at[g, block - n_seq // 2], part_recv.at[g],
-            device_id={"seq": block}, device_id_type=MESH,
+            part_out.at[g, block - n_seq // 2], part_in.at[slot],
+            part_send.at[g, block - n_seq // 2], part_recv.at[slot],
+            device_id={"seq": block if to is None else to}, device_id_type=MESH,
         )
 
     def returning(g, lane, block, d):
@@ -182,10 +186,13 @@
         for d in (*range(1, n_uly), 0):
             returning(g, lane, block, d).start()
 
-    def attend(g, block, full, diagonal, finish):
+    def attend(g, block, full, diagonal, finish, resume=None):
         for a in range(2):
             query = heads[Q, g, block, a * half:(a + 1) * half, :]
             top = total = acc = None
+            if resume is not None:
+                cut = slice(a * half, (a + 1) * half)
+                top, total, acc = own_stat[resume, 0:1, cut], own_stat[resume, 1:2, cut], own[resume, :, cut]
             spans = [(j, rows, False) for j in full] + ([(block, (a + 1) * half, True)] if diagonal else [])
             for j, count, masked in spans:
                 key = heads[K, g, j, 0:count, :]
@@ -236,85 +243,96 @@
             part_out[g, where, HEAD_DIM:HEAD_DIM + STAT, cut] = stats.astype(jnp.bfloat16)
         return finish
 
-    def merge(g):
-        pltpu.make_async_copy(part_in.at[g], part_in.at[g], part_recv.at[g]).wait()
+    def merge(g, slot=None, lane=0):
+        slot = g if slot is None else slot
+        pltpu.make_async_copy(part_in.at[slot], part_in.at[slot], part_recv.at[slot]).wait()
         for a in range(2):
             cut = slice(a * half, (a + 1) * half)
-            stats = part_in[g, HEAD_DIM:HEAD_DIM + STAT, cut].astype(jnp.float32)
+            stats = part_in[slot, HEAD_DIM:HEAD_DIM + STAT, cut].astype(jnp.float32)
             level = stats[0:1] + stats[1:2] + stats[2:3]
-            top, total = own_stat[g, 0:1, cut], own_stat[g, 1:2, cut]
+            top, total = own_stat[slot, 0:1, cut], own_stat[slot, 1:2, cut]
             new_top = jnp.maximum(top, level)
             mine, theirs = jnp.exp2(top - new_top), jnp.exp2(level - new_top)
             inverse = 1.0 / (total * mine + theirs)
-            other = part_in[g, 0:HEAD_DIM, cut].astype(jnp.float32)
-            both = own[g, :, cut] * (mine * inverse) + other * (theirs * inverse)
-            att[0, g, cut, :] = jnp.transpose(both).astype(jnp.bfloat16)
-
-    def each(count, body):
+            other = part_in[slot, 0:HEAD_DIM, cut].astype(jnp.float32)
+            both = own[slot, :, cut] * (mine * inverse) + other * (theirs * inverse)
+            att[lane, g, cut, :] = jnp.transpose(both).astype(jnp.bfloat16)
+
+    def each(first, count, body):
         def step(g, carry):
             body(g)
             return carry
-        lax.fori_loop(0, count, step, 0)
-
-    every = (alone, *range(shared))
+        lax.fori_loop(first, count, step, 0)
+
+    upward = (*range(shared - 1), alone, shared - 1)
 
     @pl.when(s == 0)
     def _():
-        for g in every:
+        for g in upward:
             scatter(K, g)
             scatter(V, g)
-        for g in every:
+        for g in upward:
             scatter(Q, g)
-        for g in every:
+        for g in upward:
             for kind in (K, V):
                 arrived(kind, g, 0)
-                if g == alone:
-                    line(kind, g, 2, 1).start()
-                else:
-                    line(kind, g, 1).start()
-        for kind in (K, V):
-            line(kind, alone, 1).start()
+                line(kind, g, 1).start()
 
         def work(g):
             arrived(Q, g, 0)
             attend(g, 0, (), True, settle(g))
             give_back(g)
-        each(group, work)
+        each(0, group, work)
 
     @pl.when(s == 1)
     def _():
-        for g in every:
+        scatter(K, alone)
+        scatter(V, alone)
+        for g in range(shared):
             scatter(K, g)
             scatter(V, g)
-        for g in every:
+        for g in range(group):
             scatter(Q, g)
         for kind in (K, V):
             arrived(kind, alone, 1)
             line(kind, alone, 2).start()
 
-        def far(g):
+        def far(g, last=3, slot=None):
             for kind in (K, V):
                 arrived(kind, g, 1)
                 arrived(kind, g, 0)
             for block in (2, 3):
                 arrived(Q, g, block)
                 attend(g, block, (0, 1), False, hand_over(g, block - n_seq // 2))
-                partial(g, block).start()
-        each(shared, far)
-        for kind in (K, V):
-            arrived(kind, alone, 0)
-
+                if block == 3:
+                    partial(g, block, last, slot).start()
+                else:
+                    partial(g, block).start()
         def near(g):
             arrived(Q, g, 1)
             attend(g, 1, (0,), True, settle(g))
             give_back(g)
-        each(group, near)
+        if guest == shared - 1:
+            for kind in (K, V):
+                arrived(kind, alone, 0)
+                line(kind, alone, 2, 1, 0).start()
+        far(guest, 2, visit)
+        each(1, shared - 1, far)
+        each(0, shared - 1, near)
+        if guest < shared - 1:
+            for kind in (K, V):
+                arrived(kind, alone, 0)
+                line(kind, alone, 2, 1, 0).start()
+        each(alone, group, near)
+        if guest < shared - 1:
+            far(shared - 1)
+        each(shared - 1, shared, near)
 
     @pl.when(s == 2)
     def _():
         for g in range(shared):
             scatter(Q, g)
-        for g in range(shared):
+        for g in (*range(1, shared), guest):
             scatter(K, g)
             scatter(V, g)
         for kind in (Q, K, V):
@@ -322,43 +340,62 @@
         for g in range(shared):
             arrived(Q, g, 2)
             line(Q, g, 1).start()
-        for g in range(shared):
-            for kind in (K, V):
-                arrived(kind, g, 2)
-                line(kind, g, 3).start()
+            arrived(Q, g, 3)
+            line(Q, g, 1, 1, 3).start()
+            if g > 0:
+                for kind in (K, V):
+                    arrived(kind, g, 2)
+                    line(kind, g, 3).start()
+        for kind in (K, V):
+            arrived(kind, guest, 2)
 
         def near(g):
             attend(g, 2, (), True, keep(g))
-        each(shared, near)
-        for kind in (Q, K, V):
-            arrived(kind, alone, 2)
-        for kind in (K, V):
-            arrived(kind, alone, 0)
-            arrived(kind, alone, 1)
-        attend(alone, 2, (0, 1), True, settle(alone))
-        give_back(alone)
-        for kind in (Q, K, V):
-            arrived(kind, alone, 3)
-        attend(alone, 3, (0, 1, 2), True, settle(alone, 1))
-        give_back(alone, 1, 3)
+        each(0, shared, near)
+        for kind in (K, V):
+            arrived(kind, guest, 3)
+        attend(guest, 3, (2,), True, keep(visit))
 
         def join(g):
             merge(g)
             give_back(g)
-        each(shared, join)
+        join(guest)
+        for kind in (K, V):
+            arrived(kind, alone, 1)
+        for kind in (Q, K, V):
+            arrived(kind, alone, 2)
+        attend(alone, 2, (1,), True, keep(alone))
+        merge(guest, visit, 1)
+        give_back(guest, 1, 3)
+        for kind in (Q, K, V):
+            arrived(kind, alone, 3)
+        attend(alone, 3, (1, 2), True, keep(late))
+        each(1, shared - 1, join)
+        for kind in (K, V):
+            arrived(kind, alone, 0)
+        attend(alone, 3, (0,), False, settle(alone, 1), late)
+        give_back(alone, 1, 3)
+        attend(alone, 2, (0,), False, settle(alone), alone)
+        give_back(alone)
+        each(max(1, shared - 1), shared, join)
 
     @pl.when(s == 3)
     def _():
         for g in range(shared):
             scatter(Q, g)
+        for kind in (K, V):
+            scatter(kind, guest)
+        for g in range(1, shared):
+            scatter(K, g)
+            scatter(V, g)
         for kind in (Q, K, V):
             scatter(kind, alone)
         for g in range(shared):
-            scatter(K, g)
-            scatter(V, g)
-        for g in range(shared):
             arrived(Q, g, 3)
-            line(Q, g, 1).start()
+            line(Q, g, 2).start()
+        for kind in (K, V):
+            arrived(kind, guest, 3)
+            line(kind, guest, 2).start()
         for kind in (Q, K, V):
             arrived(kind, alone, 3)
             line(kind, alone, 2).start()
@@ -368,12 +405,12 @@
                 arrived(kind, g, 3)
                 arrived(kind, g, 2)
             attend(g, 3, (2,), True, keep(g))
-        each(shared, near)
+        each(1, shared, near)
 
         def join(g):
             merge(g)
             give_back(g)
-        each(shared, join)
+        each(1, shared, join)
 
     past_load.wait()
     weights = [table_ref[0, slot_ref[p]] + table_ref[1, slot_ref[p]] for p in range(past.shape[0])]
@@ -386,7 +423,7 @@
             for p, weight in enumerate(weights):
                 mixed = mixed + weight * past[p, :, cols].astype(jnp.float32)
             out_ref[:, cols] = mixed.astype(out_ref.dtype)
-    each(group, combine)
+    each(0, group, combine)
 
     for g in range(group):
         for d in range(1, n_uly):
@@ -403,13 +440,12 @@
             for kind in (K, V):
                 line(kind, g, 1).wait_send()
             returned(g)
-        for kind in (K, V):
-            line(kind, alone, 2, 1).wait_send()
 
     @pl.when(s == 1)
     def _():
         for kind in (K, V):
             line(kind, alone, 2).wait_send()
+            line(kind, alone, 2, 1, 0).wait_send()
         for g in range(shared):
             for block in (2, 3):
                 partial(g, block).wait_send()
@@ -420,16 +456,22 @@
     def _():
         for g in range(shared):
             line(Q, g, 1).wait_send()
+            line(Q, g, 1, 1, 3).wait_send()
+        for g in range(1, shared):
             for kind in (K, V):
                 line(kind, g, 3).wait_send()
         for g in range(group):
             returned(g)
-        returned(alone, 1, 3)
+        for g in (guest, alone):
+            returned(g, 1, 3)
 
     @pl.when(s == 3)
     def _():
         for g in range(shared):
-            line(Q, g, 1).wait_send()
+            line(Q, g, 2).wait_send()
+        for kind in (K, V):
+            line(kind, guest, 2).wait_send()
+        for g in range(1, shared):
             returned(g)
         for kind in (Q, K, V):
             line(kind, alone, 2).wait_send()
@@ -453,10 +495,10 @@
             pltpu.VMEM((3, tokens, features), bf16),
             pltpu.VMEM((stored, tokens, features), bf16),
             pltpu.VMEM((3, group, n_seq, rows, HEAD_DIM), bf16),
-            pltpu.VMEM((group, HEAD_DIM, rows), f32),
-            pltpu.VMEM((group, 8, rows), f32),
+            pltpu.VMEM((group + 2, HEAD_DIM, rows), f32),
+            pltpu.VMEM((group + 2, 8, rows), f32),
             pltpu.VMEM((group, 2, HEAD_DIM + STAT, rows), bf16),
-            pltpu.VMEM((group, HEAD_DIM + STAT, rows), bf16),
+            pltpu.VMEM((group + 2, HEAD_DIM + STAT, rows), bf16),
             pltpu.VMEM((2, group, rows, HEAD_DIM), bf16),
             pltpu.VMEM((tokens, features), bf16),
             pltpu.SemaphoreType.DMA((3,)),
@@ -465,18 +507,22 @@
             pltpu.SemaphoreType.DMA((3, group, 2)),
             pltpu.SemaphoreType.DMA((3, group, n_seq)),
             pltpu.SemaphoreType.DMA((group, 2)),
-            pltpu.SemaphoreType.DMA((group,)),
+            pltpu.SemaphoreType.DMA((group + 2,)),
             pltpu.SemaphoreType.DMA((2, group, n_uly)),
             pltpu.SemaphoreType.DMA((group, n_uly)),
         ],
         compiler_params=pltpu.CompilerParams(
-            collective_id=0, has_side_effects=True, vmem_limit_bytes=48 * 1024 * 1024
+            collective_id=0, has_side_effects=True, vmem_limit_bytes=62 * 1024 * 1024
         ),
     )(dwa_slot, dwa_table, queries, keys, values, past_outputs)
 
 
 def solution(mesh):
-    body = fused if mesh.shape["seq"] == SPAN else shards
+    def body(queries, *rest):
+        heads_here = queries.shape[1] // HEAD_DIM // mesh.shape["uly"]
+        fits = mesh.shape["seq"] == SPAN and heads_here >= 2
+        return (fused if fits else shards)(queries, *rest)
+
     return jax.shard_map(
         body,
         mesh=mesh,

time: 55.3 us -> 50.2 us (0.908)
  local copies, waits for them, and re-layouts: 6.48 us -> 1.88 us
    unnamed x13 -> x1, local copies, waits for them, and re-layouts: 6.48 us -> 1.88 us
where the time goes in v2:
time: 50.2 us; the launch traced here: 49.9 us
  Pallas kernels  48 us (96%)
  local copies, waits for them, and re-layouts  1.88 us (4%)
    pallas_call x1, Pallas kernels, fused(): pl.pallas_call(functools.partial(fused_kernel, (n_seq, n_uly, group)), ou...  48 us
    unnamed x1, local copies, waits for them, and re-layouts  1.88 us

profile of v2, /device:TPU:24, one launch (start us, length us, event | category | flops | bytes accessed | tf_op | source)
XLA Modules:
  0.0 49.9 jit_solution(17910245695502481137)
XLA Ops:
  0.0 48.0 %shard_map.64 = bf16[128,2048]{1,0:T(8,128)(2,1)} custom-call(s32[2]{0:T(128)} %slot_ref.1, f32[2,64]{1,0:T(2,128)} %table_ref.1, bf16[128,2048]{1,0:T(8,128)(2,1)} %q_hbm.1, bf16[128,2048]{1,0:T(8,128)(2,1)} %k_hbm.1, bf16[128,2048]{1,0:T(8,128)(2,1)} %v_hbm.1, bf16[2,128,2048]{2,1,0:T(8,128)(2,1)} %past_hbm.1), custom_call_target="tpu_custom_call" | custom-call | tf_op jit(solution)/shard_map/pallas_call | solution.py:489
  48.0 1.9 %copy.8 = bf16[128,2048]{1,0:T(8,128)(2,1)} copy(bf16[128,2048]{1,0:T(8,128)(2,1)} %shard_map.64) | data formatting | bytes 1048576

commit v3 on v2

--- a/solution.py
+++ b/solution.py
@@ -301,7 +301,7 @@
             for kind in (K, V):
                 arrived(kind, g, 1)
                 arrived(kind, g, 0)
-            for block in (2, 3):
+            for block in (3, 2):
                 arrived(Q, g, block)
                 attend(g, block, (0, 1), False, hand_over(g, block - n_seq // 2))
                 if block == 3:
@@ -423,7 +423,9 @@
             for p, weight in enumerate(weights):
                 mixed = mixed + weight * past[p, :, cols].astype(jnp.float32)
             out_ref[:, cols] = mixed.astype(out_ref.dtype)
-    each(0, group, combine)
+    each(0, shared - 1, combine)
+    each(alone, group, combine)
+    each(shared - 1, shared, combine)
 
     for g in range(group):
         for d in range(1, n_uly):

time: 50.2 us -> 51.1 us (1.018)
  the two profiles are of different devices: /device:TPU:24 before, /device:TPU:16 now
where the time goes in v3:
time: 51.1 us; the launch traced here: 51 us
  Pallas kernels  49.1 us (96%)
  local copies, waits for them, and re-layouts  1.88 us (4%)
    pallas_call x1, Pallas kernels, fused(): pl.pallas_call(functools.partial(fused_kernel, (n_seq, n_uly, group)), ou...  49.1 us
    unnamed x1, local copies, waits for them, and re-layouts  1.88 us

profile of v3, /device:TPU:16, one launch (start us, length us, event | category | flops | bytes accessed | tf_op | source)
XLA Modules:
  0.0 51.0 jit_solution(17871492389666819426)
XLA Ops:
  0.0 49.1 %shard_map.64 = bf16[128,2048]{1,0:T(8,128)(2,1)} custom-call(s32[2]{0:T(128)} %slot_ref.1, f32[2,64]{1,0:T(2,128)} %table_ref.1, bf16[128,2048]{1,0:T(8,128)(2,1)} %q_hbm.1, bf16[128,2048]{1,0:T(8,128)(2,1)} %k_hbm.1, bf16[128,2048]{1,0:T(8,128)(2,1)} %v_hbm.1, bf16[2,128,2048]{2,1,0:T(8,128)(2,1)} %past_hbm.1), custom_call_target="tpu_custom_call" | custom-call | tf_op jit(solution)/shard_map/pallas_call | solution.py:491
  49.1 1.9 %copy.8 = bf16[128,2048]{1,0:T(8,128)(2,1)} copy(bf16[128,2048]{1,0:T(8,128)(2,1)} %shard_map.64) | data formatting | bytes 1048576
